TPU v7x, 256 devices: a whole 4x4x8 slice. The times are simulated.
256 devices in a mesh: loop: 256 (over z, y, x, core).
Axes of the slice: x: 4, y: 4, z: 8, core: 2. Of those that a mesh axis runs over, the one named last changes fastest.
Arguments:
- signal: float32 [256, 8192, 256], P('loop'), may hold values from -8 to 8, as said below
- tap_gain: float32 [3, 256], replicated, may hold values from 0.3 to 1.2
Outputs:
- filtered: float32 [256, 8192, 256], P('loop')
Inputs may be any that keep to these rules, and one draw needn't show every extreme that they name: signal holds numbers from -8 to 8.
All inputs are finite; a program needn't handle non-finite values.
Results may differ from a plain program's by a relative error of at most 0.0003.
Values sent between devices are 32-bit elements.
A program may use at most 64 MiB of HBM per device.

v0:
```python
import jax
import jax.numpy as jnp
from jax import lax
from jax.sharding import PartitionSpec as P


def passed_along(value, axis, steps):
    count = lax.axis_size(axis)
    pairs = [(source, (source + steps) % count) for source in range(count)]
    return lax.ppermute(value, axis, pairs)


def body(signal, tap_gain):
    wide_in = signal.astype(jnp.float32)
    copy_1 = passed_along(signal, "loop", 33)
    copy_2 = passed_along(signal, "loop", 127)
    mixed = (
        tap_gain[0] * wide_in
        + tap_gain[1] * copy_1.astype(jnp.float32)
        + tap_gain[2] * copy_2.astype(jnp.float32)
    )
    filtered = jnp.tanh(mixed).astype(jnp.float32)
    return filtered


def solution(mesh):
    return jax.shard_map(
        body,
        mesh=mesh,
        in_specs=(P("loop", None, None), P()),
        out_specs=P("loop", None, None),
        check_vma=False,
    )
```

profile of v0, /device:TPU:31, one launch (start us, length us, event | category | flops | bytes accessed | tf_op | source)
XLA Modules:
  0.0 660.1 jit_solution(12470322294750838387)
XLA Ops:
  0.0 7.5 %collective-permute-start.1 = (f32[1,8192,256]{2,1,0:T(8,128)}, f32[1,8192,256]{2,1,0:T(8,128)S(1)}, u32[]{:S(2)}, u32[]{:S(2)}) collective-permute-start(f32[1,8192,256]{2,1,0:T(8,128)} %param.2), channel_id=1, source_target_pairs={{0,127},{1,128},{2,129},{3,130},{4,131},{5,132},{6,133},{7,134},{8... | collective-permute-start | bytes 25165832 | tf_op jit(solution)/shard_map/ppermute | solution.py:10
  7.5 4.7 collective-permute-start
  12.1 0.8 fusion
  12.9 533.9 %collective-permute-done.1 = f32[1,8192,256]{2,1,0:T(8,128)S(1)} collective-permute-done((f32[1,8192,256]{2,1,0:T(8,128)}, f32[1,8192,256]{2,1,0:T(8,128)S(1)}, u32[]{:S(2)}, u32[]{:S(2)}) %collective-permute-start.1) | collective-permute-done | bytes 8388640 | tf_op jit(solution)/shard_map/ppermute | solution.py:10
  546.9 106.6 %collective-permute-done = f32[1,8192,256]{2,1,0:T(8,128)S(1)} collective-permute-done((f32[1,8192,256]{2,1,0:T(8,128)}, f32[1,8192,256]{2,1,0:T(8,128)S(1)}, u32[]{:S(2)}, u32[]{:S(2)}) %collective-permute-start) | collective-permute-done | bytes 8388640 | tf_op jit(solution)/shard_map/ppermute | solution.py:10
  653.5 6.5 add_tanh_fusion
Async XLA Ops:
  0.0 546.9 %collective-permute-start.1 = (f32[1,8192,256]{2,1,0:T(8,128)}, f32[1,8192,256]{2,1,0:T(8,128)S(1)}, u32[]{:S(2)}, u32[]{:S(2)}) collective-permute-start(f32[1,8192,256]{2,1,0:T(8,128)} %param.2), channel_id=1, source_target_pairs={{0,127},{1,128},{2,129},{3,130},{4,131},{5,132},{6,133},{7,134},{8... | collective-permute-start | bytes 25165832 | tf_op jit(solution)/shard_map/ppermute | solution.py:10
  7.5 646.0 %collective-permute-start = (f32[1,8192,256]{2,1,0:T(8,128)}, f32[1,8192,256]{2,1,0:T(8,128)S(1)}, u32[]{:S(2)}, u32[]{:S(2)}) collective-permute-start(f32[1,8192,256]{2,1,0:T(8,128)} %param.2), channel_id=1, source_target_pairs={{0,33},{1,34},{2,35},{3,36},{4,37},{5,38},{6,39},{7,40},{8,41},{9,... | collective-permute-start | bytes 25165832 | tf_op jit(solution)/shard_map/ppermute | solution.py:10
where the time goes:
time: 665 us; the launch traced here: 660 us
  waiting for transfers between devices  641 us (96%)
  starting transfers between devices  12.1 us (2%)
    ppermute x2, waiting for transfers between devices, passed_along(): return lax.ppermute(value, axis, pairs)  641 us
  transfers between devices with their start and end apart: 2, of which 2 were waited for; matrix products, arithmetic and copies ran while one was open for 0% of the time, Pallas kernels for 0%

commit v1 on v0

v1 whole, which is shorter than its diff:
```python
import functools

import jax
import jax.numpy as jnp
from jax import lax
from jax.experimental import pallas as pl
from jax.experimental.pallas import tpu as pltpu
from jax.sharding import PartitionSpec as P

AXIS = "loop"
NEAR, FAR = 33, 127
HOP = FAR - NEAR - NEAR
BACK_1, BACK_2 = 64, 65
PLANE = 32
NC = 16
DIVERTED = NC * 3 // 4
PARTNERS = (NEAR, HOP, BACK_1, BACK_2, 31, 2, 125)


def kernel(count, x_hbm, gain, out, x, d, g, m, q, b, relay, load_sem, send_sem,
           d_sem, g_sem, m_sem, q_sem, b_sem, relay_sem):
    me = lax.axis_index(AXIS)
    r = lax.rem(me, PLANE)
    half = x_hbm.shape[1] // 2
    cr = half // NC

    def away(steps):
        return lax.rem(me + steps + count, count)

    def cls(u):
        return lax.rem(u // 2, 2)

    ahead = cls(me)
    back = 1 - ahead
    summed = cls(away(-FAR))

    barrier = pltpu.get_barrier_semaphore()
    for steps in PARTNERS:
        for sign in (1, -1):
            pl.semaphore_signal(barrier, inc=1, device_id=away(sign * steps),
                                device_id_type=pl.DeviceIdType.LOGICAL)
    pl.semaphore_wait(barrier, 2 * len(PARTNERS))

    def rows(i):
        return pl.ds(pl.multiple_of(i * cr, cr), cr)

    def rows_of(which, i):
        return pl.ds(pl.multiple_of(which * half + i * cr, cr), cr)

    def send(src, dst, flow, sem, steps):
        pltpu.make_async_remote_copy(
            src_ref=src, dst_ref=dst, send_sem=send_sem.at[flow], recv_sem=sem,
            device_id=away(steps), device_id_type=pl.DeviceIdType.LOGICAL,
        ).start()

    def arrived(buf, sem, i):
        pltpu.make_async_copy(buf.at[rows(i)], buf.at[rows(i)], sem.at[i]).wait()

    loads = pltpu.make_async_copy(x_hbm.at[0], x, load_sem)
    n_back = jnp.where(r == 0, DIVERTED, NC)

    def first(i, carry):
        src = x_hbm.at[0, rows_of(ahead, i)]

        @pl.when(r == PLANE - 1)
        def _():
            send(src, relay.at[rows(i)], 0, relay_sem.at[i], 1 - PLANE)

        @pl.when(r != PLANE - 1)
        def _():
            send(src, d.at[rows(i)], 0, d_sem.at[i], NEAR)

        other = x_hbm.at[0, rows_of(back, i)]

        @pl.when(i < n_back)
        def _():
            send(other, q.at[rows(i)], 1, q_sem.at[i], -BACK_1)

        @pl.when(i >= n_back)
        def _():
            send(other, relay.at[rows(i)], 1, relay_sem.at[i], 2)

        return carry

    lax.fori_loop(0, NC, first, 0)
    loads.start()

    def second(i, carry):
        @pl.when(r == 0)
        def _():
            arrived(relay, relay_sem, i)
            send(relay.at[rows(i)], d.at[rows(i)], 5, d_sem.at[i], 2 * PLANE)

        @pl.when((r == 2) & (i >= DIVERTED))
        def _():
            arrived(relay, relay_sem, i)
            send(relay.at[rows(i)], b.at[rows(i)], 5, b_sem.at[i], 125)

        arrived(d, d_sem, i)
        send(d.at[rows(i)], g.at[rows(i)], 2, g_sem.at[i], HOP)
        return carry

    lax.fori_loop(0, NC, second, 0)

    def turn(i, carry):
        arrived(q, q_sem, i)
        send(q.at[rows(i)], b.at[rows(i)], 3, b_sem.at[i], -BACK_2)
        return carry

    lax.fori_loop(0, n_back, turn, 0)
    loads.wait()
    g0, g1, g2 = gain[0:1, :], gain[1:2, :], gain[2:3, :]

    def merge(i, carry):
        arrived(g, g_sem, i)
        g[rows(i), :] = g2 * g[rows(i), :] + g1 * x[rows_of(back, i), :]

        @pl.when(i > 0)
        def _():
            send(g.at[rows(i - 1)], m.at[rows(i - 1)], 4, m_sem.at[i - 1], NEAR)

        return carry

    lax.fori_loop(0, NC, merge, 0)
    send(g.at[rows(NC - 1)], m.at[rows(NC - 1)], 4, m_sem.at[NC - 1], NEAR)

    def finish(i, carry):
        arrived(b, b_sem, i)
        plain = rows_of(1 - summed, i)
        out[0, plain, :] = jnp.tanh(g0 * x[plain, :] + g1 * d[rows(i), :] + g2 * b[rows(i), :])
        arrived(m, m_sem, i)
        ready = rows_of(summed, i)
        out[0, ready, :] = jnp.tanh(g0 * x[ready, :] + m[rows(i), :])
        return carry

    lax.fori_loop(0, NC, finish, 0)

    def sent(flow, n):
        size = pl.ds(0, n * cr)
        pltpu.make_async_copy(q.at[size], q.at[size], send_sem.at[flow]).wait()

    for flow in (0, 1, 2, 4):
        sent(flow, NC)

    @pl.when(r == 0)
    def _():
        sent(3, DIVERTED)
        sent(5, NC)

    @pl.when(r != 0)
    def _():
        sent(3, NC)

    @pl.when(r == 2)
    def _():
        sent(5, NC - DIVERTED)


def body(count, signal, tap_gain):
    _, steps, channels = signal.shape
    block = pltpu.VMEM((steps // 2, channels), jnp.float32)
    return pl.pallas_call(
        functools.partial(kernel, count),
        out_shape=jax.ShapeDtypeStruct(signal.shape, jnp.float32),
        in_specs=[pl.BlockSpec(memory_space=pl.ANY), pl.BlockSpec(memory_space=pltpu.VMEM)],
        out_specs=pl.BlockSpec(memory_space=pltpu.VMEM),
        scratch_shapes=[
            pltpu.VMEM((steps, channels), jnp.float32),
            block, block, block, block, block, block,
            pltpu.SemaphoreType.DMA,
            pltpu.SemaphoreType.DMA((6,)),
        ] + [pltpu.SemaphoreType.DMA((NC,))] * 6,
        compiler_params=pltpu.CompilerParams(
            collective_id=0, has_side_effects=True, vmem_limit_bytes=60 << 20
        ),
    )(signal, tap_gain)


def solution(mesh):
    count = mesh.shape[AXIS]
    return jax.shard_map(
        functools.partial(body, count),
        mesh=mesh,
        in_specs=(P(AXIS, None, None), P()),
        out_specs=P(AXIS, None, None),
        check_vma=False,
    )
```

time: 665 us -> 467 us (0.70)
  waiting for transfers between devices: 641 us -> 0 us
  Pallas kernels: 0 us -> 460 us
  starting transfers between devices: 12.1 us -> 0 us
    ppermute x2 -> x0, waiting for transfers between devices: 641 us -> none  [passed_along(): return lax.ppermute(value, axis, pairs)]
    pallas_call x0 -> x1, Pallas kernels: none -> 460 us  [body(): pl.pallas_call(functools.partial(kernel, count), out_shape=jax.ShapeDtype...]
    ppermute x2 -> x0, starting transfers between devices: 12.1 us -> none  [passed_along(): return lax.ppermute(value, axis, pairs)]
    unnamed x0 -> x1, local copies, waits for them, and re-layouts: none -> 7.32 us
  transfers between devices with their start and end apart: 2 -> 0, of which waited for: 2 -> 0; matrix products, arithmetic and copies ran while one was open for 0% -> 0% of each run, Pallas kernels for 0% -> 0%
where the time goes in v1:
time: 467 us
  Pallas kernels  460 us (99%)
  local copies, waits for them, and re-layouts  7.32 us (2%)
    pallas_call x1, Pallas kernels, body(): pl.pallas_call(functools.partial(kernel, count), out_shape=jax.ShapeDtype...  460 us

profile of v1, /device:TPU:31, one launch (start us, length us, event | category | flops | bytes accessed | tf_op | source)
XLA Modules:
  0.0 467.3 jit_solution(1916565291661963191)
XLA Ops:
  0.0 460.0 %shard_map.28 = f32[1,8192,256]{2,1,0:T(8,128)} custom-call(f32[1,8192,256]{2,1,0:T(8,128)} %x_hbm.1, f32[3,256]{1,0:T(4,128)} %gain.1), custom_call_target="tpu_custom_call" | custom-call | tf_op jit(solution)/shard_map/pallas_call | solution.py:162
  460.0 7.3 %copy.4 = f32[1,8192,256]{2,1,0:T(8,128)} copy(f32[1,8192,256]{2,1,0:T(8,128)} %shard_map.28) | data formatting | bytes 16777216

commit v2 on v1

--- a/solution.py
+++ b/solution.py
@@ -59,17 +59,7 @@
     loads = pltpu.make_async_copy(x_hbm.at[0], x, load_sem)
     n_back = jnp.where(r == 0, DIVERTED, NC)
 
-    def first(i, carry):
-        src = x_hbm.at[0, rows_of(ahead, i)]
-
-        @pl.when(r == PLANE - 1)
-        def _():
-            send(src, relay.at[rows(i)], 0, relay_sem.at[i], 1 - PLANE)
-
-        @pl.when(r != PLANE - 1)
-        def _():
-            send(src, d.at[rows(i)], 0, d_sem.at[i], NEAR)
-
+    def backward(i, carry):
         other = x_hbm.at[0, rows_of(back, i)]
 
         @pl.when(i < n_back)
@@ -82,10 +72,17 @@
 
         return carry
 
-    lax.fori_loop(0, NC, first, 0)
-    loads.start()
+    def forward(i, carry):
+        src = x_hbm.at[0, rows_of(ahead, i)]
 
-    def second(i, carry):
+        @pl.when(r == PLANE - 1)
+        def _():
+            send(src, relay.at[rows(i)], 0, relay_sem.at[i], 1 - PLANE)
+
+        @pl.when(r != PLANE - 1)
+        def _():
+            send(src, d.at[rows(i)], 0, d_sem.at[i], NEAR)
+
         @pl.when(r == 0)
         def _():
             arrived(relay, relay_sem, i)
@@ -96,18 +93,23 @@
             arrived(relay, relay_sem, i)
             send(relay.at[rows(i)], b.at[rows(i)], 5, b_sem.at[i], 125)
 
+        return carry
+
+    def onward(i, carry):
         arrived(d, d_sem, i)
         send(d.at[rows(i)], g.at[rows(i)], 2, g_sem.at[i], HOP)
+
+        @pl.when(i < n_back)
+        def _():
+            arrived(q, q_sem, i)
+            send(q.at[rows(i)], b.at[rows(i)], 3, b_sem.at[i], -BACK_2)
+
         return carry
 
-    lax.fori_loop(0, NC, second, 0)
-
-    def turn(i, carry):
-        arrived(q, q_sem, i)
-        send(q.at[rows(i)], b.at[rows(i)], 3, b_sem.at[i], -BACK_2)
-        return carry
-
-    lax.fori_loop(0, n_back, turn, 0)
+    lax.fori_loop(0, NC, backward, 0)
+    lax.fori_loop(0, NC, forward, 0)
+    loads.start()
+    lax.fori_loop(0, NC, onward, 0)
     loads.wait()
     g0, g1, g2 = gain[0:1, :], gain[1:2, :], gain[2:3, :]
 

time: 467 us -> 385 us (0.82)
  Pallas kernels: 460 us -> 374 us
    pallas_call x1, Pallas kernels: 460 us -> 374 us  [body(): pl.pallas_call(functools.partial(kernel, count), out_shape=jax.ShapeDtype...]
where the time goes in v2:
time: 385 us; the launch traced here: 381 us
  Pallas kernels  374 us (97%)
  local copies, waits for them, and re-layouts  7.32 us (2%)
    pallas_call x1, Pallas kernels, body(): pl.pallas_call(functools.partial(kernel, count), out_shape=jax.ShapeDtype...  374 us

profile of v2, /device:TPU:31, one launch (start us, length us, event | category | flops | bytes accessed | tf_op | source)
XLA Modules:
  0.0 380.9 jit_solution(10522918307879246757)
XLA Ops:
  0.0 373.6 %shard_map.28 = f32[1,8192,256]{2,1,0:T(8,128)} custom-call(f32[1,8192,256]{2,1,0:T(8,128)} %x_hbm.1, f32[3,256]{1,0:T(4,128)} %gain.1), custom_call_target="tpu_custom_call" | custom-call | tf_op jit(solution)/shard_map/pallas_call | solution.py:164
  373.6 7.3 %copy.4 = f32[1,8192,256]{2,1,0:T(8,128)} copy(f32[1,8192,256]{2,1,0:T(8,128)} %shard_map.28) | data formatting | bytes 16777216

commit v3 on v2

--- a/solution.py
+++ b/solution.py
@@ -163,7 +163,7 @@
     block = pltpu.VMEM((steps // 2, channels), jnp.float32)
     return pl.pallas_call(
         functools.partial(kernel, count),
-        out_shape=jax.ShapeDtypeStruct(signal.shape, jnp.float32),
+        out_shape=pltpu.VMEM(signal.shape, jnp.float32),
         in_specs=[pl.BlockSpec(memory_space=pl.ANY), pl.BlockSpec(memory_space=pltpu.VMEM)],
         out_specs=pl.BlockSpec(memory_space=pltpu.VMEM),
         scratch_shapes=[
@@ -173,7 +173,7 @@
             pltpu.SemaphoreType.DMA((6,)),
         ] + [pltpu.SemaphoreType.DMA((NC,))] * 6,
         compiler_params=pltpu.CompilerParams(
-            collective_id=0, has_side_effects=True, vmem_limit_bytes=60 << 20
+            collective_id=0, has_side_effects=True, vmem_limit_bytes=50 << 20
         ),
     )(signal, tap_gain)
 

time: 385 us -> 378 us (0.982)
  Pallas kernels: 374 us -> 370 us
  local copies, waits for them, and re-layouts: 7.32 us -> 3.4 us
    unnamed x1, local copies, waits for them, and re-layouts: 7.32 us -> 3.4 us
where the time goes in v3:
time: 378 us; the launch traced here: 374 us
  Pallas kernels  370 us (98%)
    pallas_call x1, Pallas kernels, body(): pl.pallas_call(functools.partial(kernel, count), out_shape=pltpu.VMEM(sig...  370 us

profile of v3, /device:TPU:31, one launch (start us, length us, event | category | flops | bytes accessed | tf_op | source)
XLA Modules:
  0.0 373.8 jit_solution(16848017472525598025)
XLA Ops:
  0.0 370.4 %shard_map.28 = f32[1,8192,256]{2,1,0:T(8,128)S(1)} custom-call(f32[1,8192,256]{2,1,0:T(8,128)} %x_hbm.1, f32[3,256]{1,0:T(4,128)} %gain.1), custom_call_target="tpu_custom_call" | custom-call | tf_op jit(solution)/shard_map/pallas_call | solution.py:164
  370.4 3.4 copy.4

commit v4 on v3

--- a/solution.py
+++ b/solution.py
@@ -12,12 +12,12 @@
 HOP = FAR - NEAR - NEAR
 BACK_1, BACK_2 = 64, 65
 PLANE = 32
-NC = 16
+NC = 8
 DIVERTED = NC * 3 // 4
-PARTNERS = (NEAR, HOP, BACK_1, BACK_2, 31, 2, 125)
-
-
-def kernel(count, x_hbm, gain, out, x, d, g, m, q, b, relay, load_sem, send_sem,
+MOVED = NC // 8
+
+
+def kernel(count, x_hbm, gain, out, x, d, g, m, q, b, relay, load_sem, send_sem, ready,
            d_sem, g_sem, m_sem, q_sem, b_sem, relay_sem):
     me = lax.axis_index(AXIS)
     r = lax.rem(me, PLANE)
@@ -35,11 +35,32 @@
     summed = cls(away(-FAR))
 
     barrier = pltpu.get_barrier_semaphore()
-    for steps in PARTNERS:
-        for sign in (1, -1):
-            pl.semaphore_signal(barrier, inc=1, device_id=away(sign * steps),
-                                device_id_type=pl.DeviceIdType.LOGICAL)
-    pl.semaphore_wait(barrier, 2 * len(PARTNERS))
+
+    def tell(sem, steps):
+        pl.semaphore_signal(sem, inc=1, device_id=away(steps),
+                            device_id_type=pl.DeviceIdType.LOGICAL)
+
+    for steps in (-NEAR, BACK_1, -BACK_1, BACK_1 - HOP, BACK_2 - BACK_1):
+        tell(barrier, steps)
+
+    @pl.when(r == 0)
+    def _():
+        tell(barrier, PLANE - 1)
+        tell(barrier, 2 - 2 * PLANE)
+
+    @pl.when(r == 2)
+    def _():
+        tell(barrier, -2)
+        tell(barrier, PLANE - 3)
+
+    @pl.when(r == PLANE - 1)
+    def _():
+        tell(barrier, -FAR + 2)
+
+    more = jnp.where(r == 0, 1, jnp.where((r == 2) | (r == PLANE - 1), 2, 0))
+    pl.semaphore_wait(barrier, 5 + more)
+    tell(ready, BACK_1)
+    tell(ready, -BACK_1)
 
     def rows(i):
         return pl.ds(pl.multiple_of(i * cr, cr), cr)
@@ -77,16 +98,22 @@
 
         @pl.when(r == PLANE - 1)
         def _():
-            send(src, relay.at[rows(i)], 0, relay_sem.at[i], 1 - PLANE)
+            by = jnp.where(i < MOVED, 3 - PLANE, 1 - PLANE)
+            send(src, relay.at[rows(i)], 0, relay_sem.at[i], by)
 
         @pl.when(r != PLANE - 1)
         def _():
             send(src, d.at[rows(i)], 0, d_sem.at[i], NEAR)
 
-        @pl.when(r == 0)
+        @pl.when((r == 0) & (i >= MOVED))
         def _():
             arrived(relay, relay_sem, i)
             send(relay.at[rows(i)], d.at[rows(i)], 5, d_sem.at[i], 2 * PLANE)
+
+        @pl.when((r == 2) & (i < MOVED))
+        def _():
+            arrived(relay, relay_sem, i)
+            send(relay.at[rows(i)], d.at[rows(i)], 5, d_sem.at[i], 2 * PLANE - 2)
 
         @pl.when((r == 2) & (i >= DIVERTED))
         def _():
@@ -109,6 +136,7 @@
     lax.fori_loop(0, NC, backward, 0)
     lax.fori_loop(0, NC, forward, 0)
     loads.start()
+    pl.semaphore_wait(ready, 2)
     lax.fori_loop(0, NC, onward, 0)
     loads.wait()
     g0, g1, g2 = gain[0:1, :], gain[1:2, :], gain[2:3, :]
@@ -147,7 +175,7 @@
     @pl.when(r == 0)
     def _():
         sent(3, DIVERTED)
-        sent(5, NC)
+        sent(5, NC - MOVED)
 
     @pl.when(r != 0)
     def _():
@@ -155,7 +183,7 @@
 
     @pl.when(r == 2)
     def _():
-        sent(5, NC - DIVERTED)
+        sent(5, NC - DIVERTED + MOVED)
 
 
 def body(count, signal, tap_gain):
@@ -171,6 +199,7 @@
             block, block, block, block, block, block,
             pltpu.SemaphoreType.DMA,
             pltpu.SemaphoreType.DMA((6,)),
+            pltpu.SemaphoreType.REGULAR,
         ] + [pltpu.SemaphoreType.DMA((NC,))] * 6,
         compiler_params=pltpu.CompilerParams(
             collective_id=0, has_side_effects=True, vmem_limit_bytes=50 << 20

time: 378 us -> 375 us (level)
  no operation moved by 1% of the time
where the time goes in v4:
time: 375 us
  Pallas kernels  371 us (99%)
    pallas_call x1, Pallas kernels, body(): pl.pallas_call(functools.partial(kernel, count), out_shape=pltpu.VMEM(sig...  371 us

profile of v4, /device:TPU:31, one launch (start us, length us, event | category | flops | bytes accessed | tf_op | source)
XLA Modules:
  0.0 374.6 jit_solution(214892570369245557)
XLA Ops:
  0.0 371.1 %shard_map.28 = f32[1,8192,256]{2,1,0:T(8,128)S(1)} custom-call(f32[1,8192,256]{2,1,0:T(8,128)} %x_hbm.1, f32[3,256]{1,0:T(4,128)} %gain.1), custom_call_target="tpu_custom_call" | custom-call | tf_op jit(solution)/shard_map/pallas_call | solution.py:192
  371.1 3.4 copy.4

commit v5 on v4

--- a/solution.py
+++ b/solution.py
@@ -10,7 +10,8 @@
 AXIS = "loop"
 NEAR, FAR = 33, 127
 HOP = FAR - NEAR - NEAR
-BACK_1, BACK_2 = 64, 65
+BACK_1, BACK_2 = 96, 33
+VOUCH = 64
 PLANE = 32
 NC = 8
 DIVERTED = NC * 3 // 4
@@ -40,7 +41,7 @@
         pl.semaphore_signal(sem, inc=1, device_id=away(steps),
                             device_id_type=pl.DeviceIdType.LOGICAL)
 
-    for steps in (-NEAR, BACK_1, -BACK_1, BACK_1 - HOP, BACK_2 - BACK_1):
+    for steps in (-NEAR, NEAR, BACK_1, VOUCH, -VOUCH, VOUCH - HOP):
         tell(barrier, steps)
 
     @pl.when(r == 0)
@@ -58,9 +59,8 @@
         tell(barrier, -FAR + 2)
 
     more = jnp.where(r == 0, 1, jnp.where((r == 2) | (r == PLANE - 1), 2, 0))
-    pl.semaphore_wait(barrier, 5 + more)
-    tell(ready, BACK_1)
-    tell(ready, -BACK_1)
+    pl.semaphore_wait(barrier, 6 + more)
+    tell(ready, -VOUCH)
 
     def rows(i):
         return pl.ds(pl.multiple_of(i * cr, cr), cr)
@@ -126,22 +126,22 @@
         arrived(d, d_sem, i)
         send(d.at[rows(i)], g.at[rows(i)], 2, g_sem.at[i], HOP)
 
-        @pl.when(i < n_back)
-        def _():
-            arrived(q, q_sem, i)
-            send(q.at[rows(i)], b.at[rows(i)], 3, b_sem.at[i], -BACK_2)
-
         return carry
 
     lax.fori_loop(0, NC, backward, 0)
     lax.fori_loop(0, NC, forward, 0)
     loads.start()
-    pl.semaphore_wait(ready, 2)
+    pl.semaphore_wait(ready, 1)
     lax.fori_loop(0, NC, onward, 0)
     loads.wait()
     g0, g1, g2 = gain[0:1, :], gain[1:2, :], gain[2:3, :]
 
     def merge(i, carry):
+        @pl.when(i < n_back)
+        def _():
+            arrived(q, q_sem, i)
+            send(q.at[rows(i)], b.at[rows(i)], 3, b_sem.at[i], -BACK_2)
+
         arrived(g, g_sem, i)
         g[rows(i), :] = g2 * g[rows(i), :] + g1 * x[rows_of(back, i), :]
 
@@ -186,7 +186,33 @@
         sent(5, NC - DIVERTED + MOVED)
 
 
+def put(src, dst, sem):
+    parts = 8
+    size = src.shape[1] // parts
+    copies = [
+        pltpu.make_async_copy(
+            src.at[:, pl.ds(k * size, size)], dst.at[:, pl.ds(k * size, size)], sem.at[k]
+        )
+        for k in range(parts)
+    ]
+    for copy in copies:
+        copy.start()
+    for copy in copies:
+        copy.wait()
+
+
 def body(count, signal, tap_gain):
+    return pl.pallas_call(
+        put,
+        out_shape=jax.ShapeDtypeStruct(signal.shape, jnp.float32),
+        in_specs=[pl.BlockSpec(memory_space=pltpu.VMEM)],
+        out_specs=pl.BlockSpec(memory_space=pl.ANY),
+        scratch_shapes=[pltpu.SemaphoreType.DMA((8,))],
+        compiler_params=pltpu.CompilerParams(vmem_limit_bytes=1 << 20),
+    )(filtered(count, signal, tap_gain))
+
+
+def filtered(count, signal, tap_gain):
     _, steps, channels = signal.shape
     block = pltpu.VMEM((steps // 2, channels), jnp.float32)
     return pl.pallas_call(

time: 375 us -> 375 us (level)
    pallas_call x1 -> x2, Pallas kernels: 371 us -> 374 us  [the longest x1 370 us: filtered(): pl.pallas_call(functools.partial(kernel, count), out_shape=pltpu.VMEM(sig...]
where the time goes in v5:
time: 375 us; the launch traced here: 374 us
  Pallas kernels  374 us (100%)
    pallas_call x1, Pallas kernels, filtered(): pl.pallas_call(functools.partial(kernel, count), out_shape=pltpu.VMEM(sig...  370 us

profile of v5, /device:TPU:31, one launch (start us, length us, event | category | flops | bytes accessed | tf_op | source)
XLA Modules:
  0.0 373.8 jit_solution(5170741360033881119)
XLA Ops:
  0.0 370.4 %shard_map.28.src = f32[1,8192,256]{2,1,0:T(8,128)S(1)} custom-call(f32[1,8192,256]{2,1,0:T(8,128)} %x_hbm.1, f32[3,256]{1,0:T(4,128)} %gain.1), custom_call_target="tpu_custom_call" | custom-call | tf_op jit(solution)/shard_map/pallas_call | solution.py:218
  370.5 3.4 shard_map.29
